TPU v7x, 32 devices: a whole 2x2x4 slice. The times are simulated.
32 devices in a mesh: gx: 4 (over y, x), gy: 2 (over core), gz: 4 (over z).
Axes of the slice: x: 2, y: 2, z: 4, core: 2. Of those that a mesh axis runs over, the one named last changes fastest.
Arguments:
- flow_state: float32 [6, 16, 32, 512], P(None, 'gx', 'gy', 'gz'), may hold values from -6 to 6
Outputs:
- new_vorticity: float32 [3, 16, 32, 512], P(None, 'gx', 'gy', 'gz')
All inputs are finite; a program needn't handle non-finite values.
Results may differ from a plain program's by a relative error of at most 0.0001.
Values sent between devices are 32-bit elements; how exact they have to be, the bound alone decides.
A program may use at most 64 MiB of HBM per device.

v0:
```python
import jax
import jax.numpy as jnp
from jax import lax
from jax.sharding import PartitionSpec as P


def extended(array, sides, width):
    for axis, dim in sides:
        count, length = (lax.axis_size(axis), array.shape[dim])
        up = [(i, (i + 1) % count) for i in range(count)]
        down = [(j, i) for i, j in up]
        last = lax.slice_in_dim(array, length - width, length, axis=dim)
        initial = lax.slice_in_dim(array, 0, width, axis=dim)
        before = lax.ppermute(last, axis, up)
        after = lax.ppermute(initial, axis, down)
        array = jnp.concatenate([before, array, after], axis=dim)
    return array


def window(values, dimension, offset, length):
    return lax.slice_in_dim(values, offset, offset + length, axis=dimension)


def derivatives(padded, dimension, length):
    minus_two = window(padded, dimension, 0, length)
    minus_one = window(padded, dimension, 1, length)
    center = window(padded, dimension, 2, length)
    plus_one = window(padded, dimension, 3, length)
    plus_two = window(padded, dimension, 4, length)
    gradient = (8.0 * (plus_one[3:6] - minus_one[3:6]) - (plus_two[3:6] - minus_two[3:6])) / 12.0
    curvature = (
        16.0 * (plus_one[0:3] + minus_one[0:3])
        - (plus_two[0:3] + minus_two[0:3])
        - 30.0 * center[0:3]
    ) / 12.0
    return (gradient, curvature)


def on_device(flow_state):
    extent = flow_state.shape[1:]
    slabs = [
        extended(flow_state, (("gx", 1),), 2),
        extended(flow_state, (("gy", 2),), 2),
        extended(flow_state, (("gz", 3),), 2),
    ]
    vorticity = flow_state[0:3]
    gradients = []
    laplace = jnp.zeros_like(vorticity)
    for dimension in range(3):
        gradient, curvature = derivatives(slabs[dimension], dimension + 1, extent[dimension])
        gradients.append(gradient)
        laplace = laplace + curvature
    strain = jnp.zeros(extent, jnp.float32)
    for gradient in gradients:
        strain = strain + jnp.sum(gradient * gradient, axis=0)
    peak = lax.pmax(jnp.max(strain), ("gx", "gy", "gz"))
    step_size = 0.25 / jnp.maximum(1.0, jnp.sqrt(peak))
    stretch = jnp.zeros_like(vorticity)
    for dimension in range(3):
        stretch = stretch + vorticity[dimension : dimension + 1] * gradients[dimension]
    return vorticity + step_size * (stretch + 0.5 * laplace)


def solution(mesh):
    return jax.shard_map(
        on_device,
        mesh=mesh,
        in_specs=(P(None, "gx", "gy", "gz"),),
        out_specs=P(None, "gx", "gy", "gz"),
        check_vma=False,
    )
```

profile of v0, /device:TPU:0, one launch (start us, length us, event | category | flops | bytes accessed | tf_op | source)
XLA Modules:
  0.0 58.7 jit_solution(13331961383952064407)
XLA Ops:
  0.0 0.0 copy-start
  0.0 1.0 %fusion.37 = (f32[6,2,16,128]{3,2,1,0:T(8,128)S(1)}, f32[6,2,16,128]{3,2,1,0:T(8,128)S(1)}) fusion(f32[6,4,16,128]{3,2,1,0:T(8,128)} %param.1), kind=kLoop, calls=%fused_computation.68 | loop fusion | bytes 393216 | tf_op jit(solution)/shard_map/slice | solution.py:13
  1.0 3.0 %collective-permute-start.1 = (f32[6,2,16,128]{3,2,1,0:T(8,128)S(1)}, f32[6,2,16,128]{3,2,1,0:T(8,128)S(1)}, u32[]{:S(2)}, u32[]{:S(2)}) collective-permute-start(f32[6,2,16,128]{3,2,1,0:T(8,128)S(1)} %get-tuple-element.17), channel_id=1, source_target_pairs={{0,8},{8,16},{16,24},{24,0},{1,9},{9,17},{17,25},{25,1},{2,10},{10... | collective-permute-start | bytes 294920 | tf_op jit(solution)/shard_map/ppermute | solution.py:14
  4.0 0.0 copy-done
  4.0 0.1 fusion.39
  4.1 3.7 %collective-permute-start.4 = (f32[6,4,16,2]{3,2,1,0:T(8,128)S(1)}, f32[6,4,16,2]{3,2,1,0:T(8,128)S(1)}, u32[]{:S(2)}, u32[]{:S(2)}) collective-permute-start(f32[6,4,16,2]{3,2,1,0:T(8,128)S(1)} %get-tuple-element.24), channel_id=1, source_target_pairs={{1,0},{2,1},{3,2},{0,3},{5,4},{6,5},{7,6},{4,7},{9,8},{10,9},{11,1... | collective-permute-start | bytes 9224 | tf_op jit(solution)/shard_map/ppermute | solution.py:15
  7.8 0.1 collective-permute-start.2
  7.9 0.1 collective-permute-start.5
  8.0 0.4 collective-permute-start.3
  8.4 0.0 collective-permute-done.1
  8.4 1.4 %collective-permute-start = (f32[6,2,16,128]{3,2,1,0:T(8,128)S(1)}, f32[6,2,16,128]{3,2,1,0:T(8,128)S(1)}, u32[]{:S(2)}, u32[]{:S(2)}) collective-permute-start(f32[6,2,16,128]{3,2,1,0:T(8,128)S(1)} %get-tuple-element.16), channel_id=1, source_target_pairs={{8,0},{16,8},{24,16},{0,24},{9,1},{17,9},{25,17},{1,25},{10,2},{18... | collective-permute-start | bytes 294920 | tf_op jit(solution)/shard_map/ppermute | solution.py:15
  9.8 0.1 constant_dynamic-update-slice_fusion.1
  9.9 3.3 %collective-permute-done = f32[6,2,16,128]{3,2,1,0:T(8,128)S(1)} collective-permute-done((f32[6,2,16,128]{3,2,1,0:T(8,128)S(1)}, f32[6,2,16,128]{3,2,1,0:T(8,128)S(1)}, u32[]{:S(2)}, u32[]{:S(2)}) %collective-permute-start) | collective-permute-done | bytes 98336 | tf_op jit(solution)/shard_map/ppermute | solution.py:15
  13.3 0.0 collective-permute-done.4
  13.3 0.0 collective-permute-done.2
  13.4 3.6 %collective-permute-done.5 = f32[6,4,16,2]{3,2,1,0:T(8,128)S(1)} collective-permute-done((f32[6,4,16,2]{3,2,1,0:T(8,128)S(1)}, f32[6,4,16,2]{3,2,1,0:T(8,128)S(1)}, u32[]{:S(2)}, u32[]{:S(2)}) %collective-permute-start.5) | collective-permute-done | bytes 3104 | tf_op jit(solution)/shard_map/ppermute | solution.py:14
  17.0 0.0 collective-permute-done.3
  17.0 0.2 multiply_reduce_fusion.1
  17.2 0.6 %add_reduce_fusion = f32[]{:T(128)} fusion(f32[4,16,128]{2,1,0:T(8,128)S(1)} %get-tuple-element.14, f32[4,16,128]{2,1,0:T(8,128)S(1)} %get-tuple-element.7, f32[4,16,128]{2,1,0:T(8,128)S(1)} %get-tuple-element.5), kind=kLoop, calls=%fused_computation.59 | loop fusion | flops 24575 | bytes 98308 | tf_op jit(solution)/shard_map/reduce_max | solution.py:56
  17.8 39.3 %pmax.7 = f32[]{:T(128)} all-reduce(f32[]{:T(128)} %add_reduce_fusion), channel_id=1, replica_groups=mesh['gx'=4,'gy'=2,'gz'=4] {'gx','gy','gz'}, use_global_device_ids=true, to_apply=%region_4.0 | all-reduce | flops 1 | bytes 8 | tf_op jit(solution)/shard_map/pmax | solution.py:56
  57.9 0.8 %fusion.10 = f32[3,4,16,128]{3,2,1,0:T(8,128)} fusion(f32[6,4,16,128]{3,2,1,0:T(8,128)S(1)} %copy-done, f32[6,4,2,128]{3,2,1,0:T(2,128)S(1)} %collective-permute-done.3, f32[6,4,16,2]{3,2,1,0:T(8,128)S(1)} %collective-permute-done.5, f32[6,4,16,130]{3,2,1,0:T(8,128)S(1)} %constant_dynamic-update-slice_fusion.6, ...), kind=kLoop, calls=%fused_computation.22 | loop fusion | flops 761856 | bytes 1794052 | tf_op jit(solution)/shard_map/add | solution.py:61
  (7 shorter events, 0.1 us)
Async XLA Ops:
  0.0 4.0 %copy-start = (f32[6,4,16,128]{3,2,1,0:T(8,128)S(1)}, f32[6,4,16,128]{3,2,1,0:T(8,128)}, u32[]{:S(2)}) copy-start(f32[6,4,16,128]{3,2,1,0:T(8,128)} %param.1) | copy-start | bytes 589828
  1.0 7.4 %collective-permute-start.1 = (f32[6,2,16,128]{3,2,1,0:T(8,128)S(1)}, f32[6,2,16,128]{3,2,1,0:T(8,128)S(1)}, u32[]{:S(2)}, u32[]{:S(2)}) collective-permute-start(f32[6,2,16,128]{3,2,1,0:T(8,128)S(1)} %get-tuple-element.17), channel_id=1, source_target_pairs={{0,8},{8,16},{16,24},{24,0},{1,9},{9,17},{17,25},{25,1},{2,10},{10... | collective-permute-start | bytes 294920 | tf_op jit(solution)/shard_map/ppermute | solution.py:14
  4.1 9.2 %collective-permute-start.4 = (f32[6,4,16,2]{3,2,1,0:T(8,128)S(1)}, f32[6,4,16,2]{3,2,1,0:T(8,128)S(1)}, u32[]{:S(2)}, u32[]{:S(2)}) collective-permute-start(f32[6,4,16,2]{3,2,1,0:T(8,128)S(1)} %get-tuple-element.24), channel_id=1, source_target_pairs={{1,0},{2,1},{3,2},{0,3},{5,4},{6,5},{7,6},{4,7},{9,8},{10,9},{11,1... | collective-permute-start | bytes 9224 | tf_op jit(solution)/shard_map/ppermute | solution.py:15
  7.8 5.5 %collective-permute-start.2 = (f32[6,4,2,128]{3,2,1,0:T(2,128)S(1)}, f32[6,4,2,128]{3,2,1,0:T(2,128)S(1)}, u32[]{:S(2)}, u32[]{:S(2)}) collective-permute-start(f32[6,4,2,128]{3,2,1,0:T(2,128)S(1)} %get-tuple-element.22), channel_id=1, source_target_pairs={{4,0},{0,4},{5,1},{1,5},{6,2},{2,6},{7,3},{3,7},{12,8},{8,12},{13,... | collective-permute-start | bytes 73736 | tf_op jit(solution)/shard_map/ppermute | solution.py:15
  7.9 9.1 %collective-permute-start.5 = (f32[6,4,16,2]{3,2,1,0:T(8,128)S(1)}, f32[6,4,16,2]{3,2,1,0:T(8,128)S(1)}, u32[]{:S(2)}, u32[]{:S(2)}) collective-permute-start(f32[6,4,16,2]{3,2,1,0:T(8,128)S(1)} %get-tuple-element.25), channel_id=1, source_target_pairs={{0,1},{1,2},{2,3},{3,0},{4,5},{5,6},{6,7},{7,4},{8,9},{9,10},{10,1... | collective-permute-start | bytes 9224 | tf_op jit(solution)/shard_map/ppermute | solution.py:14
  8.0 9.0 %collective-permute-start.3 = (f32[6,4,2,128]{3,2,1,0:T(2,128)S(1)}, f32[6,4,2,128]{3,2,1,0:T(2,128)S(1)}, u32[]{:S(2)}, u32[]{:S(2)}) collective-permute-start(f32[6,4,2,128]{3,2,1,0:T(2,128)S(1)} %get-tuple-element.23), channel_id=1, source_target_pairs={{0,4},{4,0},{1,5},{5,1},{2,6},{6,2},{3,7},{7,3},{8,12},{12,8},{9,1... | collective-permute-start | bytes 73736 | tf_op jit(solution)/shard_map/ppermute | solution.py:14
  8.4 4.8 %collective-permute-start = (f32[6,2,16,128]{3,2,1,0:T(8,128)S(1)}, f32[6,2,16,128]{3,2,1,0:T(8,128)S(1)}, u32[]{:S(2)}, u32[]{:S(2)}) collective-permute-start(f32[6,2,16,128]{3,2,1,0:T(8,128)S(1)} %get-tuple-element.16), channel_id=1, source_target_pairs={{8,0},{16,8},{24,16},{0,24},{9,1},{17,9},{25,17},{1,25},{10,2},{18... | collective-permute-start | bytes 294920 | tf_op jit(solution)/shard_map/ppermute | solution.py:15
where the time goes:
time: 59.1 us; the launch traced here: 58.7 us
  blocking collectives  39.3 us (66%)
  starting transfers between devices  8.67 us (15%)
  waiting for transfers between devices  6.98 us (12%)
  other arithmetic  1.7 us (3%)
  local copies, waits for them, and re-layouts  1.23 us (2%)
  between operations  0.83 us (1%)
    pmax x1, blocking collectives, on_device(): peak = lax.pmax(jnp.max(strain), ('gx', 'gy', 'gz'))  39.3 us
    ppermute x3, starting transfers between devices, extended(): after = lax.ppermute(initial, axis, down)  5.16 us
    ppermute x3, waiting for transfers between devices, extended(): before = lax.ppermute(last, axis, up)  3.65 us
    ppermute x3, starting transfers between devices, extended(): before = lax.ppermute(last, axis, up)  3.51 us
    ppermute x3, waiting for transfers between devices, extended(): after = lax.ppermute(initial, axis, down)  3.34 us
  transfers between devices with their start and end apart: 6, of which 2 were waited for; matrix products, arithmetic and copies ran while one was open for 0% of the time, Pallas kernels for 0%

commit v1 on v0

v1 whole, which is shorter than its diff:
```python
import functools

import jax
import jax.numpy as jnp
from jax import lax
from jax.experimental import pallas as pl
from jax.experimental.pallas import tpu as pltpu
from jax.sharding import PartitionSpec as P

MESH = pl.DeviceIdType.MESH
AXES = ("gx", "gy", "gz")
LANES = 4


def shifted(values, side, dim):
    length = values.shape[dim]
    index = lax.broadcasted_iota(jnp.int32, values.shape, dim)
    return (
        pltpu.roll(jnp.where(index >= length - 2, side, values), 2, dim),
        pltpu.roll(jnp.where(index >= length - 1, side, values), 1, dim),
        pltpu.roll(jnp.where(index < 1, side, values), length - 1, dim),
        pltpu.roll(jnp.where(index < 2, side, values), length - 2, dim),
    )


def gradient(m2, m1, p1, p2):
    return (8.0 * (p1 - m1) - (p2 - m2)) * (1.0 / 12.0)


def curvature(m2, m1, center, p1, p2):
    return (16.0 * (p1 + m1) - (p2 + m2) - 30.0 * center) * (1.0 / 12.0)


def kernel(
    counts,
    flow_ref,
    out_ref,
    state,
    packed,
    from_down,
    from_up,
    beside,
    left,
    right,
    strain_ref,
    plane_peaks,
    line_peaks,
    load_sem,
    halo_send,
    halo_recv,
    plane_send,
    plane_recv,
    line_send,
    line_recv,
):
    nx, ny, nz = counts
    components, depth, rows, lanes = state.shape
    half = components // 2
    me = [lax.axis_index(axis) for axis in AXES]

    def peer(dx, dy, dz):
        return tuple(
            lax.rem(at + (step % count), count) for at, step, count in zip(me, (dx, dy, dz), counts)
        )

    plane = [(dx, dy, 0) for dx in range(nx) for dy in range(ny) if (dx, dy) != (0, 0)]
    line = [(0, 0, dz) for dz in range(1, nz)]

    loads = [
        pltpu.make_async_copy(flow_ref.at[part], state.at[part], load_sem.at[i])
        for i, part in enumerate((pl.ds(half, half), pl.ds(0, half)))
    ]
    for load in loads:
        load.start()
    barrier = pltpu.get_barrier_semaphore()
    for offset in plane + line:
        pl.semaphore_signal(barrier, inc=1, device_id=peer(*offset), device_id_type=MESH)

    for load in loads:
        load.wait()
    tiles = [(c, x) for c in range(components) for x in range(depth)]
    per_pack = lanes // LANES
    lane = lax.broadcasted_iota(jnp.int32, (rows, lanes), 1)
    for p in range(packed.shape[0]):
        total = jnp.zeros((rows, lanes), jnp.float32)
        for t, (c, x) in enumerate(tiles[p * per_pack : (p + 1) * per_pack]):
            moved = pltpu.roll(state[c, x], (LANES * t + 2) % lanes, 1)
            total = jnp.where(lane >= LANES * t, moved, total)
        packed[p] = total

    pl.semaphore_wait(barrier, len(plane) + len(line))

    def send(i, source, target, offset):
        copy = pltpu.make_async_remote_copy(
            src_ref=source,
            dst_ref=target,
            send_sem=halo_send.at[i],
            recv_sem=halo_recv.at[i],
            device_id=peer(*offset),
            device_id_type=MESH,
        )
        copy.start()
        return copy

    velocity, vorticity = pl.ds(half, half), pl.ds(0, half)
    u_copies = [
        send(0, state.at[velocity, pl.ds(depth - 2, 2)], left.at[velocity], (1, 0, 0)),
        send(1, state.at[velocity, pl.ds(0, 2)], right.at[velocity], (-1, 0, 0)),
    ]
    near_copies = [
        send(2, packed, from_down, (0, 0, 1)),
        send(3, packed, from_up, (0, 0, -1)),
        send(4, state.at[:, :, pl.ds(rows - 8, 8)], beside.at[:, :, pl.ds(rows - 8, 8)], (0, 1, 0)),
        send(5, state.at[:, :, pl.ds(0, 8)], beside.at[:, :, pl.ds(0, 8)], (0, -1, 0)),
    ]
    w_copies = [
        send(6, state.at[vorticity, pl.ds(depth - 2, 2)], left.at[vorticity], (1, 0, 0)),
        send(7, state.at[vorticity, pl.ds(0, 2)], right.at[vorticity], (-1, 0, 0)),
    ]

    for copy in near_copies:
        copy.wait_recv()
    sides = [
        jnp.where((lane % LANES) < 2, from_down[p], from_up[p]) for p in range(packed.shape[0])
    ]

    def z_side(c, x):
        t = c * depth + x
        return pltpu.roll(sides[t // per_pack], (lanes - (LANES * (t % per_pack) + 2)) % lanes, 1)

    for x in range(depth):
        strain = jnp.zeros((rows, lanes), jnp.float32)
        w_y, w_z = state[1, x], state[2, x]
        for c in range(half):
            u, w = state[half + c, x], state[c, x]
            grad_y = gradient(*shifted(u, beside[half + c, x], 0))
            grad_z = gradient(*shifted(u, z_side(half + c, x), 1))
            strain = strain + grad_y * grad_y + grad_z * grad_z
            m2, m1, p1, p2 = shifted(w, beside[c, x], 0)
            laplace = curvature(m2, m1, w, p1, p2)
            m2, m1, p1, p2 = shifted(w, z_side(c, x), 1)
            laplace = laplace + curvature(m2, m1, w, p1, p2)
            out_ref[c, x] = w_y * grad_y + w_z * grad_z + 0.5 * laplace
        strain_ref[x] = strain

    def layer(c, x):
        if x < 0:
            return left[c, x + 2]
        if x >= depth:
            return right[c, x - depth]
        return state[c, x]

    for copy in u_copies:
        copy.wait_recv()
    peak = jnp.zeros((rows, lanes), jnp.float32)
    for x in range(depth):
        strain = strain_ref[x]
        w_x = state[0, x]
        for c in range(half):
            grad_x = gradient(*(layer(half + c, x + k) for k in (-2, -1, 1, 2)))
            strain = strain + grad_x * grad_x
            out_ref[c, x] = out_ref[c, x] + w_x * grad_x
        peak = jnp.maximum(peak, strain)

    def spread(values, slots, offsets, send_sem, recv_sem):
        slots[0] = values
        copies = []
        for i, offset in enumerate(offsets):
            copy = pltpu.make_async_remote_copy(
                src_ref=slots.at[0],
                dst_ref=slots.at[i + 1],
                send_sem=send_sem.at[i],
                recv_sem=recv_sem.at[i],
                device_id=peer(*offset),
                device_id_type=MESH,
            )
            copy.start()
            copies.append(copy)
        return copies

    peak_copies = spread(
        jnp.max(peak, axis=0, keepdims=True), plane_peaks, plane, plane_send, plane_recv
    )
    for copy in w_copies:
        copy.wait_recv()
    for x in range(depth):
        for c in range(half):
            m2, m1, w, p1, p2 = (layer(c, x + k) for k in (-2, -1, 0, 1, 2))
            out_ref[c, x] = out_ref[c, x] + 0.5 * curvature(m2, m1, w, p1, p2)
    for copy in peak_copies:
        copy.wait_recv()
    line_copies = spread(
        jnp.max(plane_peaks[...], axis=0), line_peaks, line, line_send, line_recv
    )
    for copy in line_copies:
        copy.wait_recv()
    peak = jnp.max(jnp.max(line_peaks[...], axis=0), axis=1, keepdims=True)
    step_size = 0.25 / jnp.maximum(1.0, jnp.sqrt(peak))
    for x in range(depth):
        for c in range(half):
            out_ref[c, x] = state[c, x] + step_size * out_ref[c, x]
    for copy in u_copies + near_copies + w_copies + peak_copies + line_copies:
        copy.wait_send()


def on_device(counts, flow_state):
    components, depth, rows, lanes = flow_state.shape
    nx, ny, nz = counts
    half = components // 2
    per_pack = lanes // LANES
    packs = -(-components * depth // per_pack)
    plane, line = nx * ny - 1, nz - 1
    f32 = jnp.float32
    dma = pltpu.SemaphoreType.DMA
    return pl.pallas_call(
        functools.partial(kernel, counts),
        out_shape=jax.ShapeDtypeStruct((half, depth, rows, lanes), f32),
        in_specs=[pl.BlockSpec(memory_space=pl.ANY)],
        out_specs=pl.BlockSpec(memory_space=pltpu.VMEM),
        scratch_shapes=[
            pltpu.VMEM((components, depth, rows, lanes), f32),
            pltpu.VMEM((packs, rows, lanes), f32),
            pltpu.VMEM((packs, rows, lanes), f32),
            pltpu.VMEM((packs, rows, lanes), f32),
            pltpu.VMEM((components, depth, rows, lanes), f32),
            pltpu.VMEM((components, 2, rows, lanes), f32),
            pltpu.VMEM((components, 2, rows, lanes), f32),
            pltpu.VMEM((depth, rows, lanes), f32),
            pltpu.VMEM((plane + 1, 1, lanes), f32),
            pltpu.VMEM((line + 1, 1, lanes), f32),
            dma((2,)),
            dma((8,)),
            dma((8,)),
            dma((plane,)),
            dma((plane,)),
            dma((line,)),
            dma((line,)),
        ],
        compiler_params=pltpu.CompilerParams(collective_id=0, has_side_effects=True),
    )(flow_state)


def solution(mesh):
    counts = tuple(mesh.shape[axis] for axis in AXES)
    return jax.shard_map(
        functools.partial(on_device, counts),
        mesh=mesh,
        in_specs=(P(None, *AXES),),
        out_specs=P(None, *AXES),
        check_vma=False,
    )
```

time: 59.1 us -> 20.1 us (0.34)
  blocking collectives: 39.3 us -> 0 us
  Pallas kernels: 0 us -> 18.4 us
  starting transfers between devices: 8.67 us -> 0 us
  waiting for transfers between devices: 6.98 us -> 0 us
  other arithmetic: 1.7 us -> 0 us
  between operations: 0.83 us -> 0.01 us
    pmax x1 -> x0, blocking collectives: 39.3 us -> none  [on_device(): peak = lax.pmax(jnp.max(strain), ('gx', 'gy', 'gz'))]
    pallas_call x0 -> x1, Pallas kernels: none -> 18.4 us  [on_device(): pl.pallas_call(functools.partial(kernel, counts), out_shape=jax.ShapeDtyp...]
    ppermute x6 -> x0, starting transfers between devices: 8.67 us -> none  [the longest x3 5.16 us: extended(): after = lax.ppermute(initial, axis, down)]
    ppermute x6 -> x0, waiting for transfers between devices: 6.98 us -> none  [the longest x3 3.65 us: extended(): before = lax.ppermute(last, axis, up)]
    unnamed x4 -> x1, local copies, waits for them, and re-layouts: 0.07 us -> 1.54 us
    slice x3 -> x0, local copies, waits for them, and re-layouts: 1.12 us -> none  [extended(): initial = lax.slice_in_dim(array, 0, width, axis=dim)]
    add x1 -> x0, other arithmetic: 0.85 us -> none  [on_device(): return vorticity + step_size * (stretch + 0.5 * laplace)]
    reduce_max x1 -> x0, other arithmetic: 0.61 us -> none  [on_device(): peak = lax.pmax(jnp.max(strain), ('gx', 'gy', 'gz'))]
  transfers between devices with their start and end apart: 6 -> 0, of which waited for: 2 -> 0; matrix products, arithmetic and copies ran while one was open for 0% -> 0% of each run, Pallas kernels for 0% -> 0%
where the time goes in v1:
time: 20.1 us; the launch traced here: 20 us
  Pallas kernels  18.4 us (92%)
  local copies, waits for them, and re-layouts  1.54 us (8%)
    pallas_call x1, Pallas kernels, on_device(): pl.pallas_call(functools.partial(kernel, counts), out_shape=jax.ShapeDtyp...  18.4 us
    unnamed x1, local copies, waits for them, and re-layouts  1.54 us

profile of v1, /device:TPU:0, one launch (start us, length us, event | category | flops | bytes accessed | tf_op | source)
XLA Modules:
  0.0 20.0 jit_solution(15111314418105098433)
XLA Ops:
  0.0 18.4 %shard_map.17 = f32[3,4,16,128]{3,2,1,0:T(8,128)} custom-call(f32[6,4,16,128]{3,2,1,0:T(8,128)} %flow_ref.1), custom_call_target="tpu_custom_call" | custom-call | tf_op jit(solution)/shard_map/pallas_call | solution.py:215
  18.4 1.5 %copy.3 = f32[3,4,16,128]{3,2,1,0:T(8,128)} copy(f32[3,4,16,128]{3,2,1,0:T(8,128)} %shard_map.17) | data formatting | bytes 196608

commit v2 on v1

--- a/solution.py
+++ b/solution.py
@@ -10,6 +10,7 @@
 MESH = pl.DeviceIdType.MESH
 AXES = ("gx", "gy", "gz")
 LANES = 4
+VMEM_BYTES = 4 * 1024 * 1024
 
 
 def shifted(values, side, dim):
@@ -43,15 +44,13 @@
     left,
     right,
     strain_ref,
-    plane_peaks,
-    line_peaks,
+    peaks,
     load_sem,
     halo_send,
     halo_recv,
-    plane_send,
-    plane_recv,
-    line_send,
-    line_recv,
+    peak_send,
+    peak_recv,
+    ready,
 ):
     nx, ny, nz = counts
     components, depth, rows, lanes = state.shape
@@ -65,16 +64,17 @@
 
     plane = [(dx, dy, 0) for dx in range(nx) for dy in range(ny) if (dx, dy) != (0, 0)]
     line = [(0, 0, dz) for dz in range(1, nz)]
+    others = [(dx, dy, dz) for dz in range(1, nz) for dx in range(nx) for dy in range(ny)] + plane
 
     loads = [
         pltpu.make_async_copy(flow_ref.at[part], state.at[part], load_sem.at[i])
         for i, part in enumerate((pl.ds(half, half), pl.ds(0, half)))
     ]
+    barrier = pltpu.get_barrier_semaphore()
+    for offset in line + plane:
+        pl.semaphore_signal(barrier, inc=1, device_id=peer(*offset), device_id_type=MESH)
     for load in loads:
         load.start()
-    barrier = pltpu.get_barrier_semaphore()
-    for offset in plane + line:
-        pl.semaphore_signal(barrier, inc=1, device_id=peer(*offset), device_id_type=MESH)
 
     for load in loads:
         load.wait()
@@ -118,6 +118,9 @@
         send(7, state.at[vorticity, pl.ds(0, 2)], right.at[vorticity], (-1, 0, 0)),
     ]
 
+    for offset in plane:
+        pl.semaphore_signal(ready, inc=1, device_id=peer(*offset), device_id_type=MESH)
+
     for copy in near_copies:
         copy.wait_recv()
     sides = [
@@ -162,45 +165,36 @@
             out_ref[c, x] = out_ref[c, x] + w_x * grad_x
         peak = jnp.maximum(peak, strain)
 
-    def spread(values, slots, offsets, send_sem, recv_sem):
-        slots[0] = values
-        copies = []
-        for i, offset in enumerate(offsets):
-            copy = pltpu.make_async_remote_copy(
-                src_ref=slots.at[0],
-                dst_ref=slots.at[i + 1],
-                send_sem=send_sem.at[i],
-                recv_sem=recv_sem.at[i],
-                device_id=peer(*offset),
-                device_id_type=MESH,
-            )
-            copy.start()
-            copies.append(copy)
-        return copies
-
-    peak_copies = spread(
-        jnp.max(peak, axis=0, keepdims=True), plane_peaks, plane, plane_send, plane_recv
-    )
+    peaks[0] = jnp.max(peak, axis=0, keepdims=True)
+    pl.semaphore_wait(ready, len(plane))
+    peak_copies = []
+    for i, offset in enumerate(others):
+        copy = pltpu.make_async_remote_copy(
+            src_ref=peaks.at[0],
+            dst_ref=peaks.at[i + 1],
+            send_sem=peak_send,
+            recv_sem=peak_recv,
+            device_id=peer(*offset),
+            device_id_type=MESH,
+        )
+        copy.start()
+        peak_copies.append(copy)
     for copy in w_copies:
         copy.wait_recv()
     for x in range(depth):
         for c in range(half):
             m2, m1, w, p1, p2 = (layer(c, x + k) for k in (-2, -1, 0, 1, 2))
             out_ref[c, x] = out_ref[c, x] + 0.5 * curvature(m2, m1, w, p1, p2)
-    for copy in peak_copies:
-        copy.wait_recv()
-    line_copies = spread(
-        jnp.max(plane_peaks[...], axis=0), line_peaks, line, line_send, line_recv
-    )
-    for copy in line_copies:
-        copy.wait_recv()
-    peak = jnp.max(jnp.max(line_peaks[...], axis=0), axis=1, keepdims=True)
+    pltpu.make_async_copy(peaks.at[pl.ds(1, len(others))], peaks.at[pl.ds(1, len(others))], peak_send).wait()
+    for copy in u_copies + near_copies + w_copies:
+        copy.wait_send()
+    everyone = pltpu.make_async_copy(peaks.at[pl.ds(1, len(others))], peaks.at[pl.ds(1, len(others))], peak_recv)
+    everyone.wait()
+    peak = jnp.max(jnp.max(peaks[...], axis=0), axis=1, keepdims=True)
     step_size = 0.25 / jnp.maximum(1.0, jnp.sqrt(peak))
     for x in range(depth):
         for c in range(half):
             out_ref[c, x] = state[c, x] + step_size * out_ref[c, x]
-    for copy in u_copies + near_copies + w_copies + peak_copies + line_copies:
-        copy.wait_send()
 
 
 def on_device(counts, flow_state):
@@ -209,7 +203,7 @@
     half = components // 2
     per_pack = lanes // LANES
     packs = -(-components * depth // per_pack)
-    plane, line = nx * ny - 1, nz - 1
+    devices = nx * ny * nz
     f32 = jnp.float32
     dma = pltpu.SemaphoreType.DMA
     return pl.pallas_call(
@@ -226,17 +220,15 @@
             pltpu.VMEM((components, 2, rows, lanes), f32),
             pltpu.VMEM((components, 2, rows, lanes), f32),
             pltpu.VMEM((depth, rows, lanes), f32),
-            pltpu.VMEM((plane + 1, 1, lanes), f32),
-            pltpu.VMEM((line + 1, 1, lanes), f32),
+            pltpu.VMEM((devices, 1, lanes), f32),
             dma((2,)),
             dma((8,)),
             dma((8,)),
-            dma((plane,)),
-            dma((plane,)),
-            dma((line,)),
-            dma((line,)),
+            dma,
+            dma,
+            pltpu.SemaphoreType.REGULAR,
         ],
-        compiler_params=pltpu.CompilerParams(collective_id=0, has_side_effects=True),
+        compiler_params=pltpu.CompilerParams(collective_id=0, has_side_effects=True, vmem_limit_bytes=VMEM_BYTES),
     )(flow_state)
 
 

time: 20.1 us -> 17.2 us (0.86)
  Pallas kernels: 18.4 us -> 15.5 us
    pallas_call x1, Pallas kernels: 18.4 us -> 15.5 us  [on_device(): pl.pallas_call(functools.partial(kernel, counts), out_shape=jax.ShapeDtyp...]
    unnamed x1 -> x3, local copies, waits for them, and re-layouts: 1.54 us -> 1.57 us
where the time goes in v2:
time: 17.2 us; the launch traced here: 17.1 us
  Pallas kernels  15.5 us (90%)
  local copies, waits for them, and re-layouts  1.57 us (9%)
    pallas_call x1, Pallas kernels, on_device(): pl.pallas_call(functools.partial(kernel, counts), out_shape=jax.ShapeDtyp...  15.5 us
    unnamed x3, local copies, waits for them, and re-layouts  1.57 us

profile of v2, /device:TPU:0, one launch (start us, length us, event | category | flops | bytes accessed | tf_op | source)
XLA Modules:
  0.0 17.1 jit_solution(15967046810866562232)
XLA Ops:
  0.0 0.0 copy-start
  0.0 0.9 %copy-done = f32[6,4,16,128]{3,2,1,0:T(8,128)S(1)} copy-done((f32[6,4,16,128]{3,2,1,0:T(8,128)S(1)}, f32[6,4,16,128]{3,2,1,0:T(8,128)}, u32[]{:S(2)}) %copy-start) | copy-done | bytes 196632
  0.9 15.5 %shard_map.17 = f32[3,4,16,128]{3,2,1,0:T(8,128)S(1)} custom-call(f32[6,4,16,128]{3,2,1,0:T(8,128)S(1)} %copy-done), custom_call_target="tpu_custom_call" | custom-call | tf_op jit(solution)/shard_map/pallas_call | solution.py:209
  16.4 0.6 %copy.3 = f32[3,4,16,128]{3,2,1,0:T(8,128)} copy(f32[3,4,16,128]{3,2,1,0:T(8,128)S(1)} %shard_map.17) | data formatting | bytes 196608
Async XLA Ops:
  0.0 0.9 %copy-start = (f32[6,4,16,128]{3,2,1,0:T(8,128)S(1)}, f32[6,4,16,128]{3,2,1,0:T(8,128)}, u32[]{:S(2)}) copy-start(f32[6,4,16,128]{3,2,1,0:T(8,128)} %flow_ref.1) | copy-start | bytes 589828

commit v3 on v2

--- a/solution.py
+++ b/solution.py
@@ -113,11 +113,6 @@
         send(4, state.at[:, :, pl.ds(rows - 8, 8)], beside.at[:, :, pl.ds(rows - 8, 8)], (0, 1, 0)),
         send(5, state.at[:, :, pl.ds(0, 8)], beside.at[:, :, pl.ds(0, 8)], (0, -1, 0)),
     ]
-    w_copies = [
-        send(6, state.at[vorticity, pl.ds(depth - 2, 2)], left.at[vorticity], (1, 0, 0)),
-        send(7, state.at[vorticity, pl.ds(0, 2)], right.at[vorticity], (-1, 0, 0)),
-    ]
-
     for offset in plane:
         pl.semaphore_signal(ready, inc=1, device_id=peer(*offset), device_id_type=MESH)
 
@@ -135,15 +130,11 @@
         strain = jnp.zeros((rows, lanes), jnp.float32)
         w_y, w_z = state[1, x], state[2, x]
         for c in range(half):
-            u, w = state[half + c, x], state[c, x]
+            u = state[half + c, x]
             grad_y = gradient(*shifted(u, beside[half + c, x], 0))
             grad_z = gradient(*shifted(u, z_side(half + c, x), 1))
             strain = strain + grad_y * grad_y + grad_z * grad_z
-            m2, m1, p1, p2 = shifted(w, beside[c, x], 0)
-            laplace = curvature(m2, m1, w, p1, p2)
-            m2, m1, p1, p2 = shifted(w, z_side(c, x), 1)
-            laplace = laplace + curvature(m2, m1, w, p1, p2)
-            out_ref[c, x] = w_y * grad_y + w_z * grad_z + 0.5 * laplace
+            out_ref[c, x] = w_y * grad_y + w_z * grad_z
         strain_ref[x] = strain
 
     def layer(c, x):
@@ -179,12 +170,21 @@
         )
         copy.start()
         peak_copies.append(copy)
+    w_copies = [
+        send(6, state.at[vorticity, pl.ds(depth - 2, 2)], left.at[vorticity], (1, 0, 0)),
+        send(7, state.at[vorticity, pl.ds(0, 2)], right.at[vorticity], (-1, 0, 0)),
+    ]
     for copy in w_copies:
         copy.wait_recv()
     for x in range(depth):
         for c in range(half):
             m2, m1, w, p1, p2 = (layer(c, x + k) for k in (-2, -1, 0, 1, 2))
-            out_ref[c, x] = out_ref[c, x] + 0.5 * curvature(m2, m1, w, p1, p2)
+            laplace = curvature(m2, m1, w, p1, p2)
+            m2, m1, p1, p2 = shifted(w, beside[c, x], 0)
+            laplace = laplace + curvature(m2, m1, w, p1, p2)
+            m2, m1, p1, p2 = shifted(w, z_side(c, x), 1)
+            laplace = laplace + curvature(m2, m1, w, p1, p2)
+            out_ref[c, x] = out_ref[c, x] + 0.5 * laplace
     pltpu.make_async_copy(peaks.at[pl.ds(1, len(others))], peaks.at[pl.ds(1, len(others))], peak_send).wait()
     for copy in u_copies + near_copies + w_copies:
         copy.wait_send()

time: 17.2 us -> 16.6 us (0.965)
  Pallas kernels: 15.5 us -> 14.9 us
    pallas_call x1, Pallas kernels: 15.5 us -> 14.9 us  [on_device(): pl.pallas_call(functools.partial(kernel, counts), out_shape=jax.ShapeDtyp...]
where the time goes in v3:
time: 16.6 us; the launch traced here: 16.4 us
  Pallas kernels  14.9 us (90%)
  local copies, waits for them, and re-layouts  1.57 us (9%)
    pallas_call x1, Pallas kernels, on_device(): pl.pallas_call(functools.partial(kernel, counts), out_shape=jax.ShapeDtyp...  14.9 us
    unnamed x3, local copies, waits for them, and re-layouts  1.57 us

profile of v3, /device:TPU:0, one launch (start us, length us, event | category | flops | bytes accessed | tf_op | source)
XLA Modules:
  0.0 16.4 jit_solution(10052779975410527091)
XLA Ops:
  0.0 0.0 copy-start
  0.0 0.9 %copy-done = f32[6,4,16,128]{3,2,1,0:T(8,128)S(1)} copy-done((f32[6,4,16,128]{3,2,1,0:T(8,128)S(1)}, f32[6,4,16,128]{3,2,1,0:T(8,128)}, u32[]{:S(2)}) %copy-start) | copy-done | bytes 196632
  0.9 14.9 %shard_map.17 = f32[3,4,16,128]{3,2,1,0:T(8,128)S(1)} custom-call(f32[6,4,16,128]{3,2,1,0:T(8,128)S(1)} %copy-done), custom_call_target="tpu_custom_call" | custom-call | tf_op jit(solution)/shard_map/pallas_call | solution.py:209
  15.8 0.6 %copy.3 = f32[3,4,16,128]{3,2,1,0:T(8,128)} copy(f32[3,4,16,128]{3,2,1,0:T(8,128)S(1)} %shard_map.17) | data formatting | bytes 196608
Async XLA Ops:
  0.0 0.9 %copy-start = (f32[6,4,16,128]{3,2,1,0:T(8,128)S(1)}, f32[6,4,16,128]{3,2,1,0:T(8,128)}, u32[]{:S(2)}) copy-start(f32[6,4,16,128]{3,2,1,0:T(8,128)} %flow_ref.1) | copy-start | bytes 589828

commit v4 on v3

--- a/solution.py
+++ b/solution.py
@@ -10,7 +10,7 @@
 MESH = pl.DeviceIdType.MESH
 AXES = ("gx", "gy", "gz")
 LANES = 4
-VMEM_BYTES = 4 * 1024 * 1024
+VMEM_BYTES = 56281250
 
 
 def shifted(values, side, dim):

time: 16.6 us -> 15.7 us (0.946)
  local copies, waits for them, and re-layouts: 1.57 us -> 0.64 us
    unnamed x3 -> x1, local copies, waits for them, and re-layouts: 1.57 us -> 0.64 us
where the time goes in v4:
time: 15.7 us; the launch traced here: 15.5 us
  Pallas kernels  14.9 us (95%)
  local copies, waits for them, and re-layouts  0.64 us (4%)
    pallas_call x1, Pallas kernels, on_device(): pl.pallas_call(functools.partial(kernel, counts), out_shape=jax.ShapeDtyp...  14.9 us
    unnamed x1, local copies, waits for them, and re-layouts  0.64 us

profile of v4, /device:TPU:0, one launch (start us, length us, event | category | flops | bytes accessed | tf_op | source)
XLA Modules:
  0.0 15.5 jit_solution(9512649697616848536)
XLA Ops:
  0.0 14.9 %shard_map.17 = f32[3,4,16,128]{3,2,1,0:T(8,128)S(1)} custom-call(f32[6,4,16,128]{3,2,1,0:T(8,128)} %flow_ref.1), custom_call_target="tpu_custom_call" | custom-call | tf_op jit(solution)/shard_map/pallas_call | solution.py:209
  14.9 0.6 %copy.3 = f32[3,4,16,128]{3,2,1,0:T(8,128)} copy(f32[3,4,16,128]{3,2,1,0:T(8,128)S(1)} %shard_map.17) | data formatting | bytes 196608

commit v5 on v4

--- a/solution.py
+++ b/solution.py
@@ -146,6 +146,10 @@
 
     for copy in u_copies:
         copy.wait_recv()
+    w_copies = [
+        send(6, state.at[vorticity, pl.ds(depth - 2, 2)], left.at[vorticity], (1, 0, 0)),
+        send(7, state.at[vorticity, pl.ds(0, 2)], right.at[vorticity], (-1, 0, 0)),
+    ]
     peak = jnp.zeros((rows, lanes), jnp.float32)
     for x in range(depth):
         strain = strain_ref[x]
@@ -170,10 +174,6 @@
         )
         copy.start()
         peak_copies.append(copy)
-    w_copies = [
-        send(6, state.at[vorticity, pl.ds(depth - 2, 2)], left.at[vorticity], (1, 0, 0)),
-        send(7, state.at[vorticity, pl.ds(0, 2)], right.at[vorticity], (-1, 0, 0)),
-    ]
     for copy in w_copies:
         copy.wait_recv()
     for x in range(depth):

time: 15.7 us -> 15.7 us (level)
  no operation moved by 1% of the time
where the time goes in v5:
time: 15.7 us; the launch traced here: 15.5 us
  Pallas kernels  14.9 us (95%)
  local copies, waits for them, and re-layouts  0.64 us (4%)
    pallas_call x1, Pallas kernels, on_device(): pl.pallas_call(functools.partial(kernel, counts), out_shape=jax.ShapeDtyp...  14.9 us
    unnamed x1, local copies, waits for them, and re-layouts  0.64 us

profile of v5, /device:TPU:0, one launch (start us, length us, event | category | flops | bytes accessed | tf_op | source)
XLA Modules:
  0.0 15.5 jit_solution(8943678158679963700)
XLA Ops:
  0.0 14.9 %shard_map.17 = f32[3,4,16,128]{3,2,1,0:T(8,128)S(1)} custom-call(f32[6,4,16,128]{3,2,1,0:T(8,128)} %flow_ref.1), custom_call_target="tpu_custom_call" | custom-call | tf_op jit(solution)/shard_map/pallas_call | solution.py:209
  14.9 0.6 %copy.3 = f32[3,4,16,128]{3,2,1,0:T(8,128)} copy(f32[3,4,16,128]{3,2,1,0:T(8,128)S(1)} %shard_map.17) | data formatting | bytes 196608
